TPU v7x, 256 devices: a whole 4x4x8 slice. The times are simulated.
256 devices in a mesh: rep: 1, r: 32 (over y, z), s: 8 (over x, core).
Axes of the slice: x: 4, y: 4, z: 8, core: 2. Of those that a mesh axis runs over, the one named last changes fastest.
Arguments:
- x: bfloat16 [256, 2048, 512], P(('rep', 'r', 's'))
- dy: bfloat16 [256, 2048, 512], P(('rep', 'r', 's'))
- w_gate: bfloat16 [2, 512, 2048], P(None, 's')
- w_up: bfloat16 [2, 512, 2048], P(None, 's')
- w_down: bfloat16 [2, 2048, 512], P(None, 's')
- m_w_gate: float32 [2, 512, 2048], P(None, 's')
- m_w_up: float32 [2, 512, 2048], P(None, 's')
- m_w_down: float32 [2, 2048, 512], P(None, 's')
- v_w_gate: float32 [2, 512, 2048], P(None, 's')
- v_w_up: float32 [2, 512, 2048], P(None, 's')
- v_w_down: float32 [2, 2048, 512], P(None, 's')
Outputs:
- output 1: bfloat16 [2, 512, 2048], P('rep', 's')
- output 2: bfloat16 [2, 512, 2048], P('rep', 's')
- output 3: bfloat16 [2, 2048, 512], P('rep', 's')
- output 4: float32 [2, 512, 2048], P('rep', 's')
- output 5: float32 [2, 512, 2048], P('rep', 's')
- output 6: float32 [2, 2048, 512], P('rep', 's')
- output 7: float32 [2, 512, 2048], P('rep', 's')
- output 8: float32 [2, 512, 2048], P('rep', 's')
- output 9: float32 [2, 2048, 512], P('rep', 's')
All inputs are finite; a program needn't handle non-finite values.
Results may differ from a plain program's by a relative error of at most 0.022.
Values are sent between devices in bfloat16 or wider.
A program may use at most 768 MiB of HBM per device.

v0:
```python
import functools

import jax
import jax.numpy as jnp
from jax import lax
from jax.experimental import pallas as pl
from jax.experimental.pallas import tpu as pltpu
from jax.sharding import PartitionSpec as P

NAMES = ("w_gate", "w_up", "w_down")
MESH = pl.DeviceIdType.MESH
RING = 4


def adamw(w, m, v, g):
    m = 0.9 * m + 0.1 * g
    v = 0.95 * v + 0.05 * g * g
    step = m * lax.rsqrt(v + 1e-8) + 0.1 * w
    return (w - 0.02 * step).astype(jnp.bfloat16), m, v


class Place:
    def __init__(self, nz):
        self.nz = nz
        r, s = lax.axis_index("r"), lax.axis_index("s")
        self.y, self.z, self.x, self.core, self.s, self.r = r // nz, r % nz, s // 2, s % 2, s, r
        self.partner = {"s": 2 * self.x + 1 - self.core}

    def at_x(self, d):
        return (self.x + d) % RING

    def at_y(self, d):
        return (self.y + d) % RING

    def at_z(self, d):
        return (self.z + d) % self.nz

    def to_x(self, d):
        return {"s": 2 * self.at_x(d) + self.core}

    def to_y(self, d):
        return {"r": self.at_y(d) * self.nz + self.z}

    def to_z(self, d):
        return {"r": self.y * self.nz + self.at_z(d)}


def meet(peers):
    barrier = pltpu.get_barrier_semaphore()
    for peer in peers:
        pl.semaphore_signal(barrier, inc=1, device_id=peer, device_id_type=MESH)
    pl.semaphore_wait(barrier, len(peers))


def send(src, dst, sems, device):
    send_sem, recv_sem = sems
    return pltpu.make_async_remote_copy(
        src_ref=src, dst_ref=dst, send_sem=send_sem, recv_sem=recv_sem, device_id=device, device_id_type=MESH
    )


class Gather:
    def __init__(self, p, ins, outs, snd, rcv, loc):
        self.p, self.ins, self.outs, self.snd, self.rcv, self.loc = p, ins, outs, snd, rcv, loc

    def block(self, l, i, x, half=None):
        ref = self.outs[i].at[l, 2 * x + self.p.core]
        if half is None:
            return ref
        rows = ref.shape[0] // 2
        return ref.at[pl.ds(half * rows, rows)]

    def copy(self, l, i, k, src, dst, device):
        return send(src, dst, (self.snd.at[3 * l + i, k], self.rcv.at[3 * l + i, k]), device)

    def own(self, l, i, k):
        p = self.p
        return self.copy(l, i, k, self.ins[i].at[l], self.block(l, i, p.x), (p.to_x(1), p.to_x(-1), p.partner)[k])

    def local(self, l, i):
        return pltpu.make_async_copy(self.ins[i].at[l], self.block(l, i, self.p.x), self.loc.at[3 * l + i])

    def on(self, l, i, k):
        p = self.p
        b = self.block(l, i, p.at_x(-1 if k == 0 else 1), k)
        return self.copy(l, i, 3 + k, b, b, p.to_x(1 if k == 0 else -1))

    def over(self, l, i, k):
        p = self.p
        b = self.block(l, i, p.at_x((-1, 1, 2, 2)[k]), (None, None, 0, 1)[k])
        return self.copy(l, i, 5 + k, b, b, p.partner)

    def first(self, l, i):
        self.local(l, i).start()
        for k in range(3):
            self.own(l, i, k).start()

    def second(self, l, i):
        for k in (0, 1):
            self.own(l, i, k).wait_recv()
            self.on(l, i, k).start()
            self.over(l, i, k).start()

    def third(self, l, i):
        for k in (0, 1):
            self.on(l, i, k).wait_recv()
            self.over(l, i, 2 + k).start()

    def last(self, l, i):
        self.own(l, i, 2).wait_recv()
        for k in range(4):
            self.over(l, i, k).wait_recv()
        self.local(l, i).wait()

    def drain(self, l, i):
        for k in range(3):
            self.own(l, i, k).wait_send()
        for k in (0, 1):
            self.on(l, i, k).wait_send()
        for k in range(4):
            self.over(l, i, k).wait_send()


def pieces(rows, columns, by_rows):
    qr, qc = (rows // RING, columns) if by_rows else (rows, columns // RING)
    across = qc // 128
    return [
        [
            (slice((q * qr if by_rows else 0) + 16 * (k // across), (q * qr if by_rows else 0) + 16 * (k // across) + 16),
             slice((0 if by_rows else q * qc) + 128 * (k % across), (0 if by_rows else q * qc) + 128 * (k % across) + 128))
            for k in range(qr // 16 * across)
        ]
        for q in range(RING)
    ]


def wide(ref):
    return ref.astype(jnp.float32)


SCRATCH = ("dg", "dd", "part", "x1", "x2", "yb", "y1", "y2", "zb", "zr", "out", "sem_d", "sem_l", "sem_z")


def reduce_scratch(nz, chunks, gate_block, down_block):
    bf = functools.partial(pltpu.VMEM, dtype=jnp.bfloat16)
    piece = (48, 128)
    return [
        pltpu.VMEM((2, 2, RING) + gate_block, jnp.bfloat16),
        pltpu.VMEM((2, RING) + down_block, jnp.bfloat16),
        pltpu.VMEM((chunks, RING, RING, nz) + piece, jnp.bfloat16),
        pltpu.VMEM((chunks, 2, RING // 2, nz) + piece, jnp.bfloat16),
        pltpu.VMEM((chunks, 2, RING, nz) + piece, jnp.bfloat16),
        pltpu.VMEM((chunks, RING, nz) + piece, jnp.bfloat16),
        pltpu.VMEM((chunks, 2, nz // 2) + piece, jnp.bfloat16),
        pltpu.VMEM((chunks, 2, nz) + piece, jnp.bfloat16),
        pltpu.VMEM((chunks, nz) + piece, jnp.bfloat16),
        pltpu.VMEM((chunks, nz) + piece, jnp.bfloat16),
        pltpu.VMEM((chunks, RING, nz) + piece, jnp.bfloat16),
        pltpu.SemaphoreType.DMA((2, chunks, 3)),
        pltpu.SemaphoreType.DMA((2, chunks, 6, 2)),
        pltpu.SemaphoreType.DMA((2, chunks, 2, nz)),
    ]


class Reduce:
    def __init__(self, p, bufs, own, gate_block, down_block, finish):
        self.p, self.own, self.finish = p, own, finish
        for name, ref in zip(SCRATCH, bufs, strict=True):
            setattr(self, name, ref)
        self.down_rows = down_block[0]
        self.gate, self.down = pieces(*gate_block, False), pieces(*down_block, True)
        self.stages = [self.s0, self.s1, self.s2, self.s3, self.s4, self.s5, self.s6, self.s7, self.s8, self.s9]

    def peers(self):
        p = self.p
        return [p.partner, p.to_x(1), p.to_x(-1), p.to_y(1), p.to_y(-1)] + [p.to_z(d) for d in range(1, p.nz)]

    def link(self, h, k, way, src, dst, device):
        return send(src, dst, (self.sem_l.at[0, h, k, way], self.sem_l.at[1, h, k, way]), device)

    def d2d(self, h, core):
        own = self.own(h)
        dst = [self.dg.at[h % 2, 0], self.dg.at[h % 2, 1], self.dd.at[h % 2]]
        return [
            send(own[i](core), dst[i], (self.sem_d.at[0, h, i], self.sem_d.at[1, h, i]), self.p.partner) for i in range(3)
        ]

    def s0(self, h):
        for one in self.d2d(h, 1 - self.p.core):
            one.start()

    def xs1(self, h):
        p = self.p
        block = self.part.at[h, p.at_x(2)]
        return [
            self.link(h, 0, 0, block.at[pl.ds(0, 2)], self.x1.at[h, 0], p.to_x(1)),
            self.link(h, 0, 1, block.at[pl.ds(2, 2)], self.x1.at[h, 1], p.to_x(-1)),
        ]

    def xs2(self, h):
        p = self.p
        return [
            self.link(h, 1, 0, self.part.at[h, p.at_x(1)], self.x2.at[h, 0], p.to_x(1)),
            self.link(h, 1, 1, self.part.at[h, p.at_x(-1)], self.x2.at[h, 1], p.to_x(-1)),
        ]

    def ys1(self, h):
        p = self.p
        block, half = self.yb.at[h, p.at_y(2)], p.nz // 2
        return [
            self.link(h, 2, 0, block.at[pl.ds(0, half)], self.y1.at[h, 0], p.to_y(1)),
            self.link(h, 2, 1, block.at[pl.ds(half, half)], self.y1.at[h, 1], p.to_y(-1)),
        ]

    def ys2(self, h):
        p = self.p
        return [
            self.link(h, 3, 0, self.yb.at[h, p.at_y(1)], self.y2.at[h, 0], p.to_y(1)),
            self.link(h, 3, 1, self.yb.at[h, p.at_y(-1)], self.y2.at[h, 1], p.to_y(-1)),
        ]

    def zs(self, h, d):
        p = self.p
        to = p.at_z(d)
        return send(self.zb.at[h, to], self.zr.at[h, p.z], (self.sem_z.at[0, h, 0, to], self.sem_z.at[1, h, 0, p.z]), p.to_z(d))

    def zs_from(self, h, d):
        p = self.p
        src = p.at_z(d)
        return send(self.zb.at[h, src], self.zr.at[h, src], (self.sem_z.at[0, h, 0, src], self.sem_z.at[1, h, 0, src]), p.to_z(d))

    def za(self, h, d):
        p = self.p
        mine = self.out.at[h, p.y, p.z]
        return send(mine, mine, (self.sem_z.at[0, h, 1, p.at_z(d)], self.sem_z.at[1, h, 1, p.z]), p.to_z(d))

    def za_from(self, h, d):
        p = self.p
        src = p.at_z(d)
        piece = self.out.at[h, p.y, src]
        return send(piece, piece, (self.sem_z.at[0, h, 1, src], self.sem_z.at[1, h, 1, src]), p.to_z(d))

    def ya1(self, h, y=None):
        p = self.p
        piece = self.out.at[h, p.y]
        return [self.link(h, 4, 0, piece, piece, p.to_y(1)), self.link(h, 4, 1, piece, piece, p.to_y(-1))]

    def ya1_from(self, h):
        p = self.p
        below, above = self.out.at[h, p.at_y(-1)], self.out.at[h, p.at_y(1)]
        return [self.link(h, 4, 0, below, below, p.to_y(1)), self.link(h, 4, 1, above, above, p.to_y(-1))]

    def ya2(self, h, first, second):
        p, half = self.p, self.p.nz // 2
        a, b = self.out.at[h, first, pl.ds(0, half)], self.out.at[h, second, pl.ds(half, half)]
        return [self.link(h, 5, 0, a, a, p.to_y(1)), self.link(h, 5, 1, b, b, p.to_y(-1))]

    def s1(self, h):
        p = self.p
        for one in self.d2d(h, 1 - p.core):
            one.wait_recv()
            one.wait_send()
        own = self.own(h)

        def block(x, _):
            for i, cut in ((0, self.gate), (1, self.gate), (2, self.down)):
                mine = own[i](p.core).at[x]
                theirs = self.dd.at[h % 2, x] if i == 2 else self.dg.at[h % 2, i, x]
                for q in range(RING):
                    for k, (rows, columns) in enumerate(cut[q]):
                        total = wide(mine[rows, columns]) + wide(theirs[rows, columns])
                        self.part[h, x, q, k, 16 * i : 16 * i + 16, :] = total.astype(jnp.bfloat16)
            return 0

        lax.fori_loop(0, RING, block, 0)
        for one in self.xs1(h):
            one.start()

    def s2(self, h):
        p = self.p
        for way, one in enumerate(self.xs1(h)):
            one.wait_recv()
        for way in (0, 1):
            to = p.at_x(1 if way == 0 else -1)

            def add(k, _):
                q, kk = 2 * way + k // p.nz, k % p.nz
                total = wide(self.part[h, to, q, kk]) + wide(self.x1[h, way, k // p.nz, kk])
                self.part[h, to, q, kk] = total.astype(jnp.bfloat16)
                return 0

            lax.fori_loop(0, 2 * p.nz, add, 0)
            self.xs2(h)[way].start()

    def s3(self, h):
        p = self.p
        for one in self.xs2(h):
            one.wait_recv()

        def add(k, _):
            q, kk = k // p.nz, k % p.nz
            total = wide(self.part[h, p.x, q, kk]) + (wide(self.x2[h, 0, q, kk]) + wide(self.x2[h, 1, q, kk]))
            self.yb[h, q, kk] = total.astype(jnp.bfloat16)
            return 0

        lax.fori_loop(0, RING * p.nz, add, 0)
        for one in self.ys1(h):
            one.start()

    def s4(self, h):
        p, half = self.p, self.p.nz // 2
        for one in self.ys1(h):
            one.wait_recv()
        for way in (0, 1):
            to = p.at_y(1 if way == 0 else -1)
            for k in range(half):
                kk = way * half + k
                self.yb[h, to, kk] = (wide(self.yb[h, to, kk]) + wide(self.y1[h, way, k])).astype(jnp.bfloat16)
            self.ys2(h)[way].start()

    def s5(self, h):
        p = self.p
        for one in self.ys2(h):
            one.wait_recv()
        for k in range(p.nz):
            total = wide(self.yb[h, p.y, k]) + (wide(self.y2[h, 0, k]) + wide(self.y2[h, 1, k]))
            self.zb[h, k] = total.astype(jnp.bfloat16)
        for d in range(1, p.nz):
            self.zs(h, d).start()

    def s6(self, h):
        p = self.p
        total = wide(self.zb[h, p.z])
        for d in range(1, p.nz):
            self.zs_from(h, d).wait_recv()
            total += wide(self.zr[h, p.at_z(d)])
        self.out[h, p.y, p.z] = total.astype(jnp.bfloat16)
        for d in range(1, p.nz):
            self.za(h, d).start()

    def s7(self, h):
        for d in range(1, self.p.nz):
            self.za_from(h, d).wait_recv()
        for one in self.ya1(h):
            one.start()

    def s8(self, h):
        p = self.p
        for one in self.ya1_from(h):
            one.wait_recv()
        for one in self.ya2(h, p.at_y(-1), p.at_y(1)):
            one.start()

    def s9(self, h):
        p = self.p
        for one in self.ya2(h, p.at_y(2), p.at_y(2)):
            one.wait_recv()
        self.finish(h)

    def drain(self, h):
        p = self.p
        for one in self.xs1(h) + self.xs2(h) + self.ys1(h) + self.ys2(h):
            one.wait_send()
        for d in range(1, p.nz):
            self.zs(h, d).wait_send()
            self.za(h, d).wait_send()
        for one in self.ya1(h) + self.ya2(h, p.at_y(-1), p.at_y(1)):
            one.wait_send()

    def unpack(self, h, b, unit, outs):
        for q in range(RING):
            for k, (rows, columns) in enumerate(self.gate[q]):
                for i in (0, 1):
                    for c in range(columns.start, columns.stop, unit):
                        to = pl.ds(pl.multiple_of(2 * c + b * unit, min(unit, 128)), min(unit, 128))
                        part = slice(c - columns.start, c - columns.start + unit)
                        outs[i][rows, to] = self.out[h, q, k, 16 * i : 16 * i + 16, part]
            for k, (rows, columns) in enumerate(self.down[q]):
                to = pl.ds(pl.multiple_of(b * self.down_rows + rows.start, 16), 16)
                outs[2][to, columns] = self.out[h, q, k, 32:48, :]


def nt(a, b):
    return lax.dot_general(a, b, (((1,), (1,)), ((), ())), preferred_element_type=jnp.float32)


def nn(a, b):
    return jnp.dot(a, b, preferred_element_type=jnp.float32)


def scaled(h):
    w = wide(h)
    return w, lax.rsqrt(jnp.mean(w * w, -1, keepdims=True) + 1e-6)


class Compute:
    def __init__(self, bufs, block):
        (self.wg, self.wu, self.wd, self.h, self.dy, self.dyt, self.a, self.at, self.acc, self.act, self.dg, self.du) = bufs
        self.block = block
        self.tokens, self.d = self.h.shape
        self.unit = self.wg.shape[3] // 16

    def each(self, body):
        def go(i, _):
            body(i, pl.ds(pl.multiple_of(i * self.block, self.block), self.block))
            return 0

        lax.fori_loop(0, self.tokens // self.block, go, 0)

    def enter(self, rows):
        w, scale = scaled(self.h[rows, :])
        self.a[0, rows, :] = (w * scale).astype(jnp.bfloat16)

    def turn_dy(self, rows):
        self.dyt[:, rows] = self.dy[rows, :].T

    def turn_a(self, l, rows):
        self.at[:, rows] = self.a[l, rows, :].T

    def forward(self, rows):
        a = self.a[0, rows, :]
        total = jnp.zeros((self.block, self.d), jnp.float32)
        ff = 16 * self.unit
        for j in range(4):
            cut = slice(j * ff // 4, (j + 1) * ff // 4)
            gate = nn(a, self.wg[0, :, :, cut].reshape(self.d, -1))
            up = nn(a, self.wu[0, :, :, cut].reshape(self.d, -1))
            act = (gate * lax.logistic(gate) * up).astype(jnp.bfloat16)
            total += nn(act, self.wd[0, 2 * j : 2 * j + 2].reshape(-1, self.d))
        h = self.h[rows, :] + total.astype(jnp.bfloat16)
        self.h[rows, :] = h
        w, scale = scaled(h)
        a = (w * scale).astype(jnp.bfloat16)
        self.a[1, rows, :] = a
        self.at[:, rows] = a.T

    def tile(self, l, b, x, gate_to, up_to, down_to):
        u = self.unit
        cuts = [pl.ds(pl.multiple_of((2 * x + c) * 2 * u + b * u, min(u, 128)), u) for c in (0, 1)]
        wg, wu = (
            jnp.concatenate([w[l, :, :, cut].reshape(self.d, u) for cut in cuts], axis=1) for w in (self.wg, self.wu)
        )
        wd = self.wd[l, pl.ds(2 * x, 2), pl.ds(pl.multiple_of(b * u, min(u, 128)), u), :].reshape(2 * u, self.d)

        def tokens(i, rows):
            a, dy = self.a[l, rows, :], self.dy[rows, :]
            gate, up, dact = nn(a, wg), nn(a, wu), nt(dy, wd)
            dact = wide(dact.astype(jnp.bfloat16))
            sig = lax.logistic(gate)
            silu = gate * sig
            dg = (dact * up * (sig + silu * (1 - sig))).astype(jnp.bfloat16)
            du = (dact * silu).astype(jnp.bfloat16)
            self.act[rows, :] = (silu * up).astype(jnp.bfloat16)
            self.dg[rows, :] = dg
            self.du[rows, :] = du
            if l == 1:
                self.acc[rows, :] += nt(dg, wg) + nt(du, wu)

        self.each(tokens)
        at = self.at[...]
        for from_, to in ((self.dg, gate_to), (self.du, up_to)):
            to[:, :, :, pl.ds(pl.multiple_of(2 * x * u, min(2 * u, 128)), 2 * u)] = (
                nn(at, from_[...]).astype(jnp.bfloat16).reshape(RING, 2, self.d // 8, 2 * u)
            )
        down_to[x] = nn(self.dyt[...], self.act[...]).T.astype(jnp.bfloat16).reshape(2, u, self.d)

    def back(self, rows):
        w, scale = scaled(self.h[rows, :])
        da = wide(self.acc[rows, :].astype(jnp.bfloat16))
        dot = jnp.sum(da * w, -1, keepdims=True) * (1.0 / self.d)
        dh = da * scale - w * (scale * scale * scale * dot)
        dy = self.dy[rows, :] + dh.astype(jnp.bfloat16)
        self.dy[rows, :] = dy
        self.dyt[:, rows] = dy.T
        self.at[:, rows] = self.a[0, rows, :].T


AFTER = (0, 1, 3, 6, 7, 8, 9, 10, 11, 12)


def step_kernel(nz, block, gate_block, down_block, *refs):
    x_in, dy_in, *rest = refs
    shards, outs, rest = rest[:3], rest[3:6], rest[6:]
    bufs, (own_g, own_d), reds, (snd, rcv, loc, io) = rest[:12], rest[12:14], rest[14:28], rest[28:]
    p = Place(nz)
    comp = Compute(bufs, block)
    unit, chunks = comp.unit, 4

    def own(h):
        return (
            lambda core: own_g.at[h % 2, 0, :, core],
            lambda core: own_g.at[h % 2, 1, :, core],
            lambda core: own_d.at[h % 2, :, core],
        )

    def finish(h):
        l, b = 1 - h // 2, h % 2
        red.unpack(h, b, unit, [o.at[l] for o in outs])

    red = Reduce(p, reds, own, gate_block, down_block, finish)
    gat = Gather(p, shards, bufs[:3], snd, rcv, loc)
    into = [pltpu.make_async_copy(x_in, comp.h, io.at[0]), pltpu.make_async_copy(dy_in, comp.dy, io.at[1])]
    for one in into:
        one.start()
    meet(red.peers())
    for i in range(3):
        gat.first(0, i)
    into[0].wait()
    comp.each(lambda i, rows: comp.enter(rows))
    gat.second(0, 0)
    into[1].wait()
    comp.each(lambda i, rows: comp.turn_dy(rows))
    gat.second(0, 1)
    gat.second(0, 2)
    for i in range(3):
        gat.first(1, i)
    for i in range(3):
        gat.third(0, i)
    for i in range(3):
        gat.last(0, i)
    comp.acc[...] = jnp.zeros_like(comp.acc)

    def ahead(i, rows):
        comp.forward(rows)
        for j in range(3):
            pl.when(i == j + 1)(functools.partial(gat.second, 1, j))

    comp.each(ahead)
    for i in range(3):
        gat.third(1, i)
    for i in range(3):
        gat.last(1, i)

    def tick(t):
        for k, (stage, after) in enumerate(zip(red.stages, AFTER, strict=True)):
            at = t - 3 - after
            pl.when((at >= 0) & (at < 4 * chunks) & (at % 4 == 0))(lambda stage=stage, at=at: stage(at // 4))

    for l in (1, 0):

        def tile(n, _):
            h = n // 4
            slot = h % 2
            comp.tile(l, n // 4 - 2 * (1 - l), n % 4, own_g.at[slot, 0], own_g.at[slot, 1], own_d.at[slot])
            tick(n)
            return 0

        lax.fori_loop(8 * (1 - l), 8 * (2 - l), tile, 0)
        if l == 1:
            comp.each(lambda i, rows: comp.back(rows))

    def late(t, _):
        tick(t)
        return 0

    lax.fori_loop(16, 16 + AFTER[-1], late, 0)

    def drain(h, _):
        red.drain(h)
        return 0

    lax.fori_loop(0, chunks, drain, 0)
    for l in (0, 1):
        for i in range(3):
            gat.drain(l, i)


def compute_scratch(tokens, d, ff):
    unit = ff // 16
    bf = jnp.bfloat16
    return [
        pltpu.VMEM((2, 8, d // 8, ff), bf),
        pltpu.VMEM((2, 8, d // 8, ff), bf),
        pltpu.VMEM((2, 8, ff // 8, d), bf),
        pltpu.VMEM((tokens, d), bf),
        pltpu.VMEM((tokens, d), bf),
        pltpu.VMEM((d, tokens), bf),
        pltpu.VMEM((2, tokens, d), bf),
        pltpu.VMEM((d, tokens), bf),
        pltpu.VMEM((tokens, d), jnp.float32),
        pltpu.VMEM((tokens, 2 * unit), bf),
        pltpu.VMEM((tokens, 2 * unit), bf),
        pltpu.VMEM((tokens, 2 * unit), bf),
    ]


def gradients_of(mesh, x, dy, weights):
    nz = mesh.shape["r"] // RING
    tokens, d = x.shape
    ff = weights[0].shape[2]
    gate_block, down_block = (d // 8, ff // 2), (ff // 16, d)
    any_space, vmem = pl.BlockSpec(memory_space=pl.ANY), pl.BlockSpec(memory_space=pltpu.VMEM)
    return pl.pallas_call(
        functools.partial(step_kernel, nz, min(512, tokens // 4), gate_block, down_block),
        out_shape=[jax.ShapeDtypeStruct(w.shape, w.dtype) for w in weights],
        in_specs=[any_space] * 5,
        out_specs=[vmem] * 3,
        scratch_shapes=compute_scratch(tokens, d, ff)
        + [
            pltpu.VMEM((2, 2, RING, 2) + gate_block, jnp.bfloat16),
            pltpu.VMEM((2, RING, 2) + down_block, jnp.bfloat16),
        ]
        + reduce_scratch(nz, 4, gate_block, down_block)
        + [
            pltpu.SemaphoreType.DMA((6, 9)),
            pltpu.SemaphoreType.DMA((6, 9)),
            pltpu.SemaphoreType.DMA((6,)),
            pltpu.SemaphoreType.DMA((2,)),
        ],
        compiler_params=pltpu.CompilerParams(collective_id=0, has_side_effects=True, vmem_limit_bytes=67043328),
        name="step",
    )(x, dy, *weights)


def solution(mesh):
    def step(x, dy, *arrays):
        weights, m, v = (arrays[i : i + 3] for i in (0, 3, 6))
        gradients = [g.astype(jnp.float32) for g in gradients_of(mesh, x[0], dy[0], weights)]
        new = [adamw(w.astype(jnp.float32), m, v, g) for w, m, v, g in zip(weights, m, v, gradients, strict=True)]
        return tuple(one[which] for which in range(3) for one in new)

    states, cut = P(("rep", "r", "s"), None, None), P(None, "s", None)
    return jax.shard_map(
        step,
        mesh=mesh,
        in_specs=(states, states) + (cut,) * 9,
        out_specs=(P("rep", "s", None),) * 9,
        check_vma=False,
    )
```

profile of v0, /device:TPU:2, one launch (start us, length us, event | category | flops | bytes accessed | tf_op | source)
XLA Modules:
  0.0 233.7 jit_solution(16640575404478510658)
XLA Ops:
  0.6 225.3 %step.1 = (bf16[2,64,2048]{2,1,0:T(8,128)(2,1)}, bf16[2,64,2048]{2,1,0:T(8,128)(2,1)}, bf16[2,256,512]{2,1,0:T(8,128)(2,1)}) custom-call(bf16[2048,512]{1,0:T(8,128)(2,1)} %bitcast.2, bf16[2048,512]{1,0:T(8,128)(2,1)} %bitcast.3, bf16[2,64,2048]{2,1,0:T(8,128)(2,1)} %refs_2_.1, bf16[2,64,2048]{2,1,0:T(8,128)(2,1)} %refs_3_.1, bf16[2,256,512]{2,1,0:T(8,128)(2,1)} %refs_4_.1), custom_call_target="tpu_custom_call" | custom-call | tf_op jit(solution)/shard_map/step/pallas_call | solution.py:593
  226.0 0.0 copy-start
  226.0 0.0 copy-start.1
  226.0 0.0 copy-start.2
  226.0 0.0 copy-start.3
  226.0 5.9 %fusion.2 = (bf16[2,64,2048]{2,1,0:T(8,128)(2,1)}, f32[2,64,2048]{2,1,0:T(8,128)}, f32[2,64,2048]{2,1,0:T(8,128)}, bf16[2,64,2048]{2,1,0:T(8,128)(2,1)}, f32[2,64,2048]{2,1,0:T(8,128)}, /*index=5*/f32[2,64,2048]{2,1,0:T(8,128)}) fusion(bf16[2,64,2048]{2,1,0:T(8,128)(2,1)} %refs_2_.1, bf16[2,64,2048]{2,1,0:T(8,128)(2,1)} %get-tuple-element.12, ...), kind=kLoop, calls=%fused_computation.14 | loop fusion | flops 8388608 | bytes 11534336 | tf_op jit(solution)/shard_map/convert_element_type | solution.py:19
  231.9 0.0 copy-done
  231.9 0.0 copy-done.1
  231.9 0.0 copy-done.2
  231.9 0.0 copy-done.3
  231.9 1.8 fusion.10
Async XLA Ops:
  226.0 5.9 %copy-start = (bf16[2,256,512]{2,1,0:T(8,128)(2,1)S(1)}, bf16[2,256,512]{2,1,0:T(8,128)(2,1)}, u32[]{:S(2)}) copy-start(bf16[2,256,512]{2,1,0:T(8,128)(2,1)} %refs_4_.1) | copy-start | bytes 1572868
  226.0 5.9 %copy-start.1 = (f32[2,256,512]{2,1,0:T(8,128)S(1)}, f32[2,256,512]{2,1,0:T(8,128)}, u32[]{:S(2)}) copy-start(f32[2,256,512]{2,1,0:T(8,128)} %param.21) | copy-start | bytes 3145732
  226.0 5.9 %copy-start.2 = (f32[2,256,512]{2,1,0:T(8,128)S(1)}, f32[2,256,512]{2,1,0:T(8,128)}, u32[]{:S(2)}) copy-start(f32[2,256,512]{2,1,0:T(8,128)} %param.18) | copy-start | bytes 3145732
  226.0 5.9 %copy-start.3 = (bf16[2,256,512]{2,1,0:T(8,128)(2,1)S(1)}, bf16[2,256,512]{2,1,0:T(8,128)(2,1)}, u32[]{:S(2)}) copy-start(bf16[2,256,512]{2,1,0:T(8,128)(2,1)} %get-tuple-element.14) | copy-start | bytes 1572868
where the time goes:
time: 235 us; the launch traced here: 234 us
  Pallas kernels  225 us (96%)
  other arithmetic  7.71 us (3%)
    pallas_call x1, Pallas kernels, gradients_of(): pl.pallas_call(functools.partial(step_kernel, nz, min(512, tokens // 4),...  225 us
    convert_element_type x2, other arithmetic, adamw(): return ((w - 0.02 * step).astype(jnp.bfloat16), m, v)  7.71 us

commit v1 on v0

--- a/solution.py
+++ b/solution.py
@@ -10,6 +10,8 @@
 NAMES = ("w_gate", "w_up", "w_down")
 MESH = pl.DeviceIdType.MESH
 RING = 4
+WAYS = (0, 1)
+SPREAD = (1, 2)
 
 
 def adamw(w, m, v, g):
@@ -25,6 +27,9 @@
         r, s = lax.axis_index("r"), lax.axis_index("s")
         self.y, self.z, self.x, self.core, self.s, self.r = r // nz, r % nz, s // 2, s % 2, s, r
         self.partner = {"s": 2 * self.x + 1 - self.core}
+        self.right, self.left, self.above, self.below = self.to_x(1), self.to_x(-1), self.to_y(1), self.to_y(-1)
+        self.x_right, self.x_left, self.x_far = (self.at_x(d) for d in (1, -1, 2))
+        self.y_above, self.y_below, self.y_far = (self.at_y(d) for d in (1, -1, 2))
 
     def at_x(self, d):
         return (self.x + d) % RING
@@ -43,6 +48,14 @@
 
     def to_z(self, d):
         return {"r": self.y * self.nz + self.at_z(d)}
+
+
+def loop(stop, body, start=0):
+    def go(i, carry):
+        body(i, carry)
+        return carry
+
+    lax.fori_loop(start, stop, go, 0)
 
 
 def meet(peers):
@@ -75,19 +88,19 @@
 
     def own(self, l, i, k):
         p = self.p
-        return self.copy(l, i, k, self.ins[i].at[l], self.block(l, i, p.x), (p.to_x(1), p.to_x(-1), p.partner)[k])
+        return self.copy(l, i, k, self.ins[i].at[l], self.block(l, i, p.x), (p.right, p.left, p.partner)[k])
 
     def local(self, l, i):
         return pltpu.make_async_copy(self.ins[i].at[l], self.block(l, i, self.p.x), self.loc.at[3 * l + i])
 
     def on(self, l, i, k):
         p = self.p
-        b = self.block(l, i, p.at_x(-1 if k == 0 else 1), k)
-        return self.copy(l, i, 3 + k, b, b, p.to_x(1 if k == 0 else -1))
+        b = self.block(l, i, (p.x_left, p.x_right)[k], k)
+        return self.copy(l, i, 3 + k, b, b, (p.right, p.left)[k])
 
     def over(self, l, i, k):
         p = self.p
-        b = self.block(l, i, p.at_x((-1, 1, 2, 2)[k]), (None, None, 0, 1)[k])
+        b = self.block(l, i, (p.x_left, p.x_right, p.x_far, p.x_far)[k], (None, None, 0, 1)[k])
         return self.copy(l, i, 5 + k, b, b, p.partner)
 
     def first(self, l, i):
@@ -96,13 +109,13 @@
             self.own(l, i, k).start()
 
     def second(self, l, i):
-        for k in (0, 1):
+        for k in WAYS:
             self.own(l, i, k).wait_recv()
             self.on(l, i, k).start()
             self.over(l, i, k).start()
 
     def third(self, l, i):
-        for k in (0, 1):
+        for k in WAYS:
             self.on(l, i, k).wait_recv()
             self.over(l, i, 2 + k).start()
 
@@ -115,7 +128,7 @@
     def drain(self, l, i):
         for k in range(3):
             self.own(l, i, k).wait_send()
-        for k in (0, 1):
+        for k in WAYS:
             self.on(l, i, k).wait_send()
         for k in range(4):
             self.over(l, i, k).wait_send()
@@ -147,7 +160,7 @@
     return [
         pltpu.VMEM((2, 2, RING) + gate_block, jnp.bfloat16),
         pltpu.VMEM((2, RING) + down_block, jnp.bfloat16),
-        pltpu.VMEM((chunks, RING, RING, nz) + piece, jnp.bfloat16),
+        pltpu.VMEM((2, RING, RING, nz) + piece, jnp.bfloat16),
         pltpu.VMEM((chunks, 2, RING // 2, nz) + piece, jnp.bfloat16),
         pltpu.VMEM((chunks, 2, RING, nz) + piece, jnp.bfloat16),
         pltpu.VMEM((chunks, RING, nz) + piece, jnp.bfloat16),
@@ -173,7 +186,7 @@
 
     def peers(self):
         p = self.p
-        return [p.partner, p.to_x(1), p.to_x(-1), p.to_y(1), p.to_y(-1)] + [p.to_z(d) for d in range(1, p.nz)]
+        return [p.partner, p.right, p.left, p.above, p.below] + [p.to_z(d) for d in range(1, p.nz)]
 
     def link(self, h, k, way, src, dst, device):
         return send(src, dst, (self.sem_l.at[0, h, k, way], self.sem_l.at[1, h, k, way]), device)
@@ -191,32 +204,32 @@
 
     def xs1(self, h):
         p = self.p
-        block = self.part.at[h, p.at_x(2)]
+        block = self.part.at[h % 2, p.x_far]
         return [
-            self.link(h, 0, 0, block.at[pl.ds(0, 2)], self.x1.at[h, 0], p.to_x(1)),
-            self.link(h, 0, 1, block.at[pl.ds(2, 2)], self.x1.at[h, 1], p.to_x(-1)),
+            self.link(h, 0, 0, block.at[pl.ds(0, 2)], self.x1.at[h, 0], p.right),
+            self.link(h, 0, 1, block.at[pl.ds(2, 2)], self.x1.at[h, 1], p.left),
         ]
 
     def xs2(self, h):
         p = self.p
         return [
-            self.link(h, 1, 0, self.part.at[h, p.at_x(1)], self.x2.at[h, 0], p.to_x(1)),
-            self.link(h, 1, 1, self.part.at[h, p.at_x(-1)], self.x2.at[h, 1], p.to_x(-1)),
+            self.link(h, 1, 0, self.part.at[h % 2, p.x_right], self.x2.at[h, 0], p.right),
+            self.link(h, 1, 1, self.part.at[h % 2, p.x_left], self.x2.at[h, 1], p.left),
         ]
 
     def ys1(self, h):
         p = self.p
-        block, half = self.yb.at[h, p.at_y(2)], p.nz // 2
+        block, half = self.yb.at[h, p.y_far], p.nz // 2
         return [
-            self.link(h, 2, 0, block.at[pl.ds(0, half)], self.y1.at[h, 0], p.to_y(1)),
-            self.link(h, 2, 1, block.at[pl.ds(half, half)], self.y1.at[h, 1], p.to_y(-1)),
+            self.link(h, 2, 0, block.at[pl.ds(0, half)], self.y1.at[h, 0], p.above),
+            self.link(h, 2, 1, block.at[pl.ds(half, half)], self.y1.at[h, 1], p.below),
         ]
 
     def ys2(self, h):
         p = self.p
         return [
-            self.link(h, 3, 0, self.yb.at[h, p.at_y(1)], self.y2.at[h, 0], p.to_y(1)),
-            self.link(h, 3, 1, self.yb.at[h, p.at_y(-1)], self.y2.at[h, 1], p.to_y(-1)),
+            self.link(h, 3, 0, self.yb.at[h, p.y_above], self.y2.at[h, 0], p.above),
+            self.link(h, 3, 1, self.yb.at[h, p.y_below], self.y2.at[h, 1], p.below),
         ]
 
     def zs(self, h, d):
@@ -243,17 +256,17 @@
     def ya1(self, h, y=None):
         p = self.p
         piece = self.out.at[h, p.y]
-        return [self.link(h, 4, 0, piece, piece, p.to_y(1)), self.link(h, 4, 1, piece, piece, p.to_y(-1))]
+        return [self.link(h, 4, 0, piece, piece, p.above), self.link(h, 4, 1, piece, piece, p.below)]
 
     def ya1_from(self, h):
         p = self.p
-        below, above = self.out.at[h, p.at_y(-1)], self.out.at[h, p.at_y(1)]
-        return [self.link(h, 4, 0, below, below, p.to_y(1)), self.link(h, 4, 1, above, above, p.to_y(-1))]
+        below, above = self.out.at[h, p.y_below], self.out.at[h, p.y_above]
+        return [self.link(h, 4, 0, below, below, p.above), self.link(h, 4, 1, above, above, p.below)]
 
     def ya2(self, h, first, second):
         p, half = self.p, self.p.nz // 2
         a, b = self.out.at[h, first, pl.ds(0, half)], self.out.at[h, second, pl.ds(half, half)]
-        return [self.link(h, 5, 0, a, a, p.to_y(1)), self.link(h, 5, 1, b, b, p.to_y(-1))]
+        return [self.link(h, 5, 0, a, a, p.above), self.link(h, 5, 1, b, b, p.below)]
 
     def s1(self, h):
         p = self.p
@@ -269,10 +282,9 @@
                 for q in range(RING):
                     for k, (rows, columns) in enumerate(cut[q]):
                         total = wide(mine[rows, columns]) + wide(theirs[rows, columns])
-                        self.part[h, x, q, k, 16 * i : 16 * i + 16, :] = total.astype(jnp.bfloat16)
-            return 0
-
-        lax.fori_loop(0, RING, block, 0)
+                        self.part[h % 2, x, q, k, 16 * i : 16 * i + 16, :] = total.astype(jnp.bfloat16)
+
+        loop(RING, block)
         for one in self.xs1(h):
             one.start()
 
@@ -280,30 +292,30 @@
         p = self.p
         for way, one in enumerate(self.xs1(h)):
             one.wait_recv()
-        for way in (0, 1):
-            to = p.at_x(1 if way == 0 else -1)
+        for way in WAYS:
+            to = (p.x_right, p.x_left)[way]
 
             def add(k, _):
                 q, kk = 2 * way + k // p.nz, k % p.nz
-                total = wide(self.part[h, to, q, kk]) + wide(self.x1[h, way, k // p.nz, kk])
-                self.part[h, to, q, kk] = total.astype(jnp.bfloat16)
-                return 0
-
-            lax.fori_loop(0, 2 * p.nz, add, 0)
+                total = wide(self.part[h % 2, to, q, kk]) + wide(self.x1[h, way, k // p.nz, kk])
+                self.part[h % 2, to, q, kk] = total.astype(jnp.bfloat16)
+
+            loop(2 * p.nz, add)
             self.xs2(h)[way].start()
 
     def s3(self, h):
         p = self.p
         for one in self.xs2(h):
             one.wait_recv()
+        for one in self.xs1(h) + self.xs2(h):
+            one.wait_send()
 
         def add(k, _):
             q, kk = k // p.nz, k % p.nz
-            total = wide(self.part[h, p.x, q, kk]) + (wide(self.x2[h, 0, q, kk]) + wide(self.x2[h, 1, q, kk]))
+            total = wide(self.part[h % 2, p.x, q, kk]) + (wide(self.x2[h, 0, q, kk]) + wide(self.x2[h, 1, q, kk]))
             self.yb[h, q, kk] = total.astype(jnp.bfloat16)
-            return 0
-
-        lax.fori_loop(0, RING * p.nz, add, 0)
+
+        loop(RING * p.nz, add)
         for one in self.ys1(h):
             one.start()
 
@@ -311,8 +323,8 @@
         p, half = self.p, self.p.nz // 2
         for one in self.ys1(h):
             one.wait_recv()
-        for way in (0, 1):
-            to = p.at_y(1 if way == 0 else -1)
+        for way in WAYS:
+            to = (p.y_above, p.y_below)[way]
             for k in range(half):
                 kk = way * half + k
                 self.yb[h, to, kk] = (wide(self.yb[h, to, kk]) + wide(self.y1[h, way, k])).astype(jnp.bfloat16)
@@ -348,23 +360,23 @@
         p = self.p
         for one in self.ya1_from(h):
             one.wait_recv()
-        for one in self.ya2(h, p.at_y(-1), p.at_y(1)):
+        for one in self.ya2(h, p.y_below, p.y_above):
             one.start()
 
     def s9(self, h):
         p = self.p
-        for one in self.ya2(h, p.at_y(2), p.at_y(2)):
+        for one in self.ya2(h, p.y_far, p.y_far):
             one.wait_recv()
         self.finish(h)
 
     def drain(self, h):
         p = self.p
-        for one in self.xs1(h) + self.xs2(h) + self.ys1(h) + self.ys2(h):
+        for one in self.ys1(h) + self.ys2(h):
             one.wait_send()
         for d in range(1, p.nz):
             self.zs(h, d).wait_send()
             self.za(h, d).wait_send()
-        for one in self.ya1(h) + self.ya2(h, p.at_y(-1), p.at_y(1)):
+        for one in self.ya1(h) + self.ya2(h, p.y_below, p.y_above):
             one.wait_send()
 
     def unpack(self, h, b, unit, outs):
@@ -380,6 +392,112 @@
                 outs[2][to, columns] = self.out[h, q, k, 32:48, :]
 
 
+class Spread:
+    def __init__(self, p, ins, outs, snd, rcv, loc):
+        self.p, self.ins, self.outs, self.snd, self.rcv, self.loc = p, ins, outs, snd, rcv, loc
+
+    def block(self, l, i, x, y=None, half=None):
+        ref = self.outs[i].at[l, 2 * x + self.p.core]
+        return ref if y is None else self.part(ref, y, half)
+
+    def part(self, ref, y, half=None):
+        rows, columns = ref.shape[0] // RING, ref.shape[1] // 2
+        some = pl.ds(pl.multiple_of(y * rows, rows), rows)
+        return ref.at[some] if half is None else ref.at[some, pl.ds(half * columns, columns)]
+
+    def copy(self, l, i, k, src, dst, device):
+        n = 2 * l + i - 1
+        return send(src, dst, (self.snd.at[n, k], self.rcv.at[n, k]), device)
+
+    def local(self, l, i):
+        return pltpu.make_async_copy(self.ins[i].at[l], self.block(l, i, self.p.x), self.loc.at[3 * l + i])
+
+    def own(self, l, i):
+        return self.copy(l, i, 0, self.ins[i].at[l], self.block(l, i, self.p.x), self.p.partner)
+
+    def x1(self, l, i, way):
+        p = self.p
+        src = self.part(self.ins[i].at[l], p.y)
+        return self.copy(l, i, 1 + way, src, self.block(l, i, p.x, p.y), (p.right, p.left)[way])
+
+    def x2(self, l, i, way):
+        p = self.p
+        b = self.block(l, i, (p.x_left, p.x_right)[way], p.y, way)
+        return self.copy(l, i, 3 + way, b, b, (p.right, p.left)[way])
+
+    def y1(self, l, i, n, way):
+        p = self.p
+        b = self.block(l, i, p.at_x(n + 1), p.y)
+        return self.copy(l, i, 5 + 2 * n + way, b, b, (p.above, p.below)[way])
+
+    def y2(self, l, i, n, way):
+        p = self.p
+        b = self.block(l, i, p.at_x(n + 1), (p.y_below, p.y_above)[way], way)
+        return self.copy(l, i, 11 + 2 * n + way, b, b, (p.above, p.below)[way])
+
+    def over(self, l, i, n):
+        b = self.block(l, i, self.p.at_x(n + 1))
+        return self.copy(l, i, 17 + n, b, b, self.p.partner)
+
+    def f1(self, l, i):
+        for way in WAYS:
+            self.x1(l, i, way).start()
+        self.local(l, i).start()
+        self.own(l, i).start()
+
+    def f2(self, l, i):
+        for way in WAYS:
+            self.x1(l, i, way).wait_recv()
+            self.x2(l, i, way).start()
+            for to in (0, 1):
+                self.y1(l, i, (2, 0)[way], to).start()
+
+    def f3(self, l, i):
+        for way in WAYS:
+            self.x2(l, i, way).wait_recv()
+        for to in (0, 1):
+            self.y1(l, i, 1, to).start()
+
+    def f4(self, l, i):
+        def go(n, _):
+            for way in WAYS:
+                self.y1(l, i, (n + 2) % 3, way).wait_recv()
+                self.y2(l, i, (n + 2) % 3, way).start()
+
+        loop(3, go)
+
+    def f5(self, l, i):
+        def go(n, _):
+            for way in WAYS:
+                self.y2(l, i, (n + 2) % 3, way).wait_recv()
+            self.over(l, i, (n + 2) % 3).start()
+
+        loop(3, go)
+
+    def f6(self, l, i):
+        self.local(l, i).wait()
+        self.own(l, i).wait_recv()
+
+        def go(n, _):
+            self.over(l, i, n).wait_recv()
+
+        loop(3, go)
+
+    def drain(self, l, i):
+        self.own(l, i).wait_send()
+        for way in WAYS:
+            self.x1(l, i, way).wait_send()
+            self.x2(l, i, way).wait_send()
+
+        def go(n, _):
+            for way in WAYS:
+                self.y1(l, i, n, way).wait_send()
+                self.y2(l, i, n, way).wait_send()
+            self.over(l, i, n).wait_send()
+
+        loop(3, go)
+
+
 def nt(a, b):
     return lax.dot_general(a, b, (((1,), (1,)), ((), ())), preferred_element_type=jnp.float32)
 
@@ -395,7 +513,7 @@
 
 class Compute:
     def __init__(self, bufs, block):
-        (self.wg, self.wu, self.wd, self.h, self.dy, self.dyt, self.a, self.at, self.acc, self.act, self.dg, self.du) = bufs
+        (self.wg, self.wu, self.wd, self.h, self.dy, self.dyt, self.a, self.at, self.acc, self.act, self.dg, self.du, self.sums) = bufs
         self.block = block
         self.tokens, self.d = self.h.shape
         self.unit = self.wg.shape[3] // 16
@@ -403,9 +521,8 @@
     def each(self, body):
         def go(i, _):
             body(i, pl.ds(pl.multiple_of(i * self.block, self.block), self.block))
-            return 0
-
-        lax.fori_loop(0, self.tokens // self.block, go, 0)
+
+        loop(self.tokens // self.block, go)
 
     def enter(self, rows):
         w, scale = scaled(self.h[rows, :])
@@ -434,8 +551,9 @@
         self.a[1, rows, :] = a
         self.at[:, rows] = a.T
 
-    def tile(self, l, b, x, gate_to, up_to, down_to):
+    def tile(self, l, n, last=None):
         u = self.unit
+        b, x, slot = n // 4, n % 4, n % 2
         cuts = [pl.ds(pl.multiple_of((2 * x + c) * 2 * u + b * u, min(u, 128)), u) for c in (0, 1)]
         wg, wu = (
             jnp.concatenate([w[l, :, :, cut].reshape(self.d, u) for cut in cuts], axis=1) for w in (self.wg, self.wu)
@@ -445,24 +563,34 @@
         def tokens(i, rows):
             a, dy = self.a[l, rows, :], self.dy[rows, :]
             gate, up, dact = nn(a, wg), nn(a, wu), nt(dy, wd)
+            if last is not None:
+                self.weigh(rows, 1 - slot)
             dact = wide(dact.astype(jnp.bfloat16))
             sig = lax.logistic(gate)
             silu = gate * sig
             dg = (dact * up * (sig + silu * (1 - sig))).astype(jnp.bfloat16)
             du = (dact * silu).astype(jnp.bfloat16)
-            self.act[rows, :] = (silu * up).astype(jnp.bfloat16)
-            self.dg[rows, :] = dg
-            self.du[rows, :] = du
+            self.act[slot, rows, :] = (silu * up).astype(jnp.bfloat16)
+            self.dg[slot, rows, :] = dg
+            self.du[slot, rows, :] = du
             if l == 1:
                 self.acc[rows, :] += nt(dg, wg) + nt(du, wu)
 
         self.each(tokens)
-        at = self.at[...]
-        for from_, to in ((self.dg, gate_to), (self.du, up_to)):
-            to[:, :, :, pl.ds(pl.multiple_of(2 * x * u, min(2 * u, 128)), 2 * u)] = (
-                nn(at, from_[...]).astype(jnp.bfloat16).reshape(RING, 2, self.d // 8, 2 * u)
-            )
-        down_to[x] = nn(self.dyt[...], self.act[...]).T.astype(jnp.bfloat16).reshape(2, u, self.d)
+        if last is not None:
+            self.settle((n - 1) % 4, *last)
+
+    def weigh(self, rows, slot):
+        for j, (left, right) in enumerate(((self.at, self.dg), (self.at, self.du), (self.dyt, self.act))):
+            self.sums[j] += nn(left[:, rows], right[slot, rows, :])
+
+    def settle(self, x, gate_to, up_to, down_to):
+        u = self.unit
+        columns = pl.ds(pl.multiple_of(2 * x * u, min(2 * u, 128)), 2 * u)
+        for j, to in enumerate((gate_to, up_to)):
+            to[:, :, :, columns] = self.sums[j].astype(jnp.bfloat16).reshape(RING, 2, self.d // 8, 2 * u)
+        down_to[x] = self.sums[2].T.astype(jnp.bfloat16).reshape(2, u, self.d)
+        self.sums[...] = jnp.zeros_like(self.sums)
 
     def back(self, rows):
         w, scale = scaled(self.h[rows, :])
@@ -475,13 +603,13 @@
         self.at[:, rows] = self.a[0, rows, :].T
 
 
-AFTER = (0, 1, 3, 6, 7, 8, 9, 10, 11, 12)
+AFTER = (0, 1, 2, 5, 6, 7, 8, 9, 10, 11)
 
 
 def step_kernel(nz, block, gate_block, down_block, *refs):
     x_in, dy_in, *rest = refs
     shards, outs, rest = rest[:3], rest[3:6], rest[6:]
-    bufs, (own_g, own_d), reds, (snd, rcv, loc, io) = rest[:12], rest[12:14], rest[14:28], rest[28:]
+    bufs, (own_g, own_d), reds, (snd, rcv, loc, io, snd_y, rcv_y) = rest[:13], rest[13:15], rest[15:29], rest[29:]
     p = Place(nz)
     comp = Compute(bufs, block)
     unit, chunks = comp.unit, 4
@@ -499,70 +627,102 @@
 
     red = Reduce(p, reds, own, gate_block, down_block, finish)
     gat = Gather(p, shards, bufs[:3], snd, rcv, loc)
+    spr = Spread(p, shards, bufs[:3], snd_y, rcv_y, loc)
     into = [pltpu.make_async_copy(x_in, comp.h, io.at[0]), pltpu.make_async_copy(dy_in, comp.dy, io.at[1])]
     for one in into:
         one.start()
     meet(red.peers())
-    for i in range(3):
-        gat.first(0, i)
+    for i in SPREAD:
+        spr.f1(0, i)
     into[0].wait()
+    for i in SPREAD:
+        spr.f2(0, i)
+    gat.first(0, 0)
     comp.each(lambda i, rows: comp.enter(rows))
-    gat.second(0, 0)
+    for i in SPREAD:
+        spr.f3(0, i)
     into[1].wait()
     comp.each(lambda i, rows: comp.turn_dy(rows))
-    gat.second(0, 1)
-    gat.second(0, 2)
-    for i in range(3):
-        gat.first(1, i)
-    for i in range(3):
-        gat.third(0, i)
-    for i in range(3):
-        gat.last(0, i)
     comp.acc[...] = jnp.zeros_like(comp.acc)
+    comp.sums[...] = jnp.zeros_like(comp.sums)
+    gat.second(0, 0)
+    for i in SPREAD:
+        spr.f4(0, i)
+        spr.f1(1, i)
+    gat.third(0, 0)
+    for i in SPREAD:
+        spr.f2(1, i)
+    gat.first(1, 0)
+    for i in SPREAD:
+        spr.f5(0, i)
+    gat.last(0, 0)
+    for i in SPREAD:
+        spr.f6(0, i)
+    for i in SPREAD:
+        spr.f3(1, i)
 
     def ahead(i, rows):
         comp.forward(rows)
-        for j in range(3):
-            pl.when(i == j + 1)(functools.partial(gat.second, 1, j))
+
+        @pl.when(i == 0)
+        def _():
+            gat.second(1, 0)
+            spr.f4(1, 1)
+
+        @pl.when(i == 1)
+        def _():
+            spr.f4(1, 2)
+            gat.third(1, 0)
+
+        pl.when(i == 2)(lambda: spr.f5(1, 1))
 
     comp.each(ahead)
-    for i in range(3):
-        gat.third(1, i)
-    for i in range(3):
-        gat.last(1, i)
+    spr.f5(1, 2)
+    gat.last(1, 0)
+    for i in SPREAD:
+        spr.f6(1, i)
 
     def tick(t):
         for k, (stage, after) in enumerate(zip(red.stages, AFTER, strict=True)):
-            at = t - 3 - after
-            pl.when((at >= 0) & (at < 4 * chunks) & (at % 4 == 0))(lambda stage=stage, at=at: stage(at // 4))
+            since = t - 4 - after
+            h = 2 * (since // 8) + (since % 8) // 3
+            due = (since >= 0) & (since < 16) & ((since % 8 == 0) | (since % 8 == 3))
+            pl.when(due)(lambda stage=stage, h=h: stage(h))
+
+    def terms(n):
+        slot = n // 4 % 2
+        return own_g.at[slot, 0], own_g.at[slot, 1], own_d.at[slot]
 
     for l in (1, 0):
+        base = 8 * (1 - l)
+        comp.tile(l, 0)
 
         def tile(n, _):
-            h = n // 4
-            slot = h % 2
-            comp.tile(l, n // 4 - 2 * (1 - l), n % 4, own_g.at[slot, 0], own_g.at[slot, 1], own_d.at[slot])
-            tick(n)
-            return 0
-
-        lax.fori_loop(8 * (1 - l), 8 * (2 - l), tile, 0)
+            tick(base + n - 1)
+            comp.tile(l, n, terms(n - 1))
+
+        loop(8, tile, 1)
+        comp.each(lambda i, rows: comp.weigh(rows, 1))
+        comp.settle(3, *terms(7))
+        tick(base + 7)
         if l == 1:
             comp.each(lambda i, rows: comp.back(rows))
 
     def late(t, _):
         tick(t)
-        return 0
-
-    lax.fori_loop(16, 16 + AFTER[-1], late, 0)
+
+    loop(16 + AFTER[-1], late, 16)
 
     def drain(h, _):
         red.drain(h)
-        return 0
-
-    lax.fori_loop(0, chunks, drain, 0)
-    for l in (0, 1):
-        for i in range(3):
-            gat.drain(l, i)
+
+    loop(chunks, drain)
+    def rest(l, _):
+        gat.drain(l, 0)
+        for i in SPREAD:
+            spr.drain(l, i)
+
+    loop(2, rest)
 
 
 def compute_scratch(tokens, d, ff):
@@ -578,9 +738,10 @@
         pltpu.VMEM((2, tokens, d), bf),
         pltpu.VMEM((d, tokens), bf),
         pltpu.VMEM((tokens, d), jnp.float32),
-        pltpu.VMEM((tokens, 2 * unit), bf),
-        pltpu.VMEM((tokens, 2 * unit), bf),
-        pltpu.VMEM((tokens, 2 * unit), bf),
+        pltpu.VMEM((2, tokens, 2 * unit), bf),
+        pltpu.VMEM((2, tokens, 2 * unit), bf),
+        pltpu.VMEM((2, tokens, 2 * unit), bf),
+        pltpu.VMEM((3, d, 2 * unit), jnp.float32),
     ]
 
 
@@ -606,6 +767,8 @@
             pltpu.SemaphoreType.DMA((6, 9)),
             pltpu.SemaphoreType.DMA((6,)),
             pltpu.SemaphoreType.DMA((2,)),
+            pltpu.SemaphoreType.DMA((4, 20)),
+            pltpu.SemaphoreType.DMA((4, 20)),
         ],
         compiler_params=pltpu.CompilerParams(collective_id=0, has_side_effects=True, vmem_limit_bytes=67043328),
         name="step",

time: 235 us -> 215 us (0.915)
  Pallas kernels: 225 us -> 206 us
    pallas_call x1, Pallas kernels: 225 us -> 206 us  [gradients_of(): pl.pallas_call(functools.partial(step_kernel, nz, min(512, tokens // 4),...]
where the time goes in v1:
time: 215 us; the launch traced here: 214 us
  Pallas kernels  206 us (96%)
  other arithmetic  7.71 us (4%)
    pallas_call x1, Pallas kernels, gradients_of(): pl.pallas_call(functools.partial(step_kernel, nz, min(512, tokens // 4),...  206 us
    convert_element_type x2, other arithmetic, adamw(): return ((w - 0.02 * step).astype(jnp.bfloat16), m, v)  7.71 us

profile of v1, /device:TPU:2, one launch (start us, length us, event | category | flops | bytes accessed | tf_op | source)
XLA Modules:
  0.0 214.2 jit_solution(12262704652845440077)
XLA Ops:
  0.6 205.8 %step.1 = (bf16[2,64,2048]{2,1,0:T(8,128)(2,1)}, bf16[2,64,2048]{2,1,0:T(8,128)(2,1)}, bf16[2,256,512]{2,1,0:T(8,128)(2,1)}) custom-call(bf16[2048,512]{1,0:T(8,128)(2,1)} %bitcast.2, bf16[2048,512]{1,0:T(8,128)(2,1)} %bitcast.3, bf16[2,64,2048]{2,1,0:T(8,128)(2,1)} %refs_2_.1, bf16[2,64,2048]{2,1,0:T(8,128)(2,1)} %refs_3_.1, bf16[2,256,512]{2,1,0:T(8,128)(2,1)} %refs_4_.1), custom_call_target="tpu_custom_call" | custom-call | tf_op jit(solution)/shard_map/step/pallas_call | solution.py:754
  206.4 0.0 copy-start
  206.4 0.0 copy-start.1
  206.5 0.0 copy-start.2
  206.5 0.0 copy-start.3
  206.5 5.9 %fusion.2 = (bf16[2,64,2048]{2,1,0:T(8,128)(2,1)}, f32[2,64,2048]{2,1,0:T(8,128)}, f32[2,64,2048]{2,1,0:T(8,128)}, bf16[2,64,2048]{2,1,0:T(8,128)(2,1)}, f32[2,64,2048]{2,1,0:T(8,128)}, /*index=5*/f32[2,64,2048]{2,1,0:T(8,128)}) fusion(bf16[2,64,2048]{2,1,0:T(8,128)(2,1)} %refs_2_.1, bf16[2,64,2048]{2,1,0:T(8,128)(2,1)} %get-tuple-element.12, ...), kind=kLoop, calls=%fused_computation.14 | loop fusion | flops 8388608 | bytes 11534336 | tf_op jit(solution)/shard_map/convert_element_type | solution.py:21
  212.4 0.0 copy-done
  212.4 0.0 copy-done.1
  212.4 0.0 copy-done.2
  212.4 0.0 copy-done.3
  212.4 1.8 fusion.10
Async XLA Ops:
  206.4 5.9 %copy-start = (bf16[2,256,512]{2,1,0:T(8,128)(2,1)S(1)}, bf16[2,256,512]{2,1,0:T(8,128)(2,1)}, u32[]{:S(2)}) copy-start(bf16[2,256,512]{2,1,0:T(8,128)(2,1)} %refs_4_.1) | copy-start | bytes 1572868
  206.4 5.9 %copy-start.1 = (f32[2,256,512]{2,1,0:T(8,128)S(1)}, f32[2,256,512]{2,1,0:T(8,128)}, u32[]{:S(2)}) copy-start(f32[2,256,512]{2,1,0:T(8,128)} %param.21) | copy-start | bytes 3145732
  206.5 5.9 %copy-start.2 = (f32[2,256,512]{2,1,0:T(8,128)S(1)}, f32[2,256,512]{2,1,0:T(8,128)}, u32[]{:S(2)}) copy-start(f32[2,256,512]{2,1,0:T(8,128)} %param.18) | copy-start | bytes 3145732
  206.5 5.9 %copy-start.3 = (bf16[2,256,512]{2,1,0:T(8,128)(2,1)S(1)}, bf16[2,256,512]{2,1,0:T(8,128)(2,1)}, u32[]{:S(2)}) copy-start(bf16[2,256,512]{2,1,0:T(8,128)(2,1)} %get-tuple-element.14) | copy-start | bytes 1572868

commit v2 on v1

--- a/solution.py
+++ b/solution.py
@@ -603,7 +603,7 @@
         self.at[:, rows] = self.a[0, rows, :].T
 
 
-AFTER = (0, 1, 2, 5, 6, 7, 8, 9, 10, 11)
+AFTER = (0, 1, 2, 5, 6, 8, 10, 12, 14, 15)
 
 
 def step_kernel(nz, block, gate_block, down_block, *refs):

time: 215 us -> 215 us (level)
  no operation moved by 1% of the time
where the time goes in v2:
time: 215 us
  Pallas kernels  206 us (96%)
  other arithmetic  7.71 us (4%)
    pallas_call x1, Pallas kernels, gradients_of(): pl.pallas_call(functools.partial(step_kernel, nz, min(512, tokens // 4),...  206 us
    convert_element_type x2, other arithmetic, adamw(): return ((w - 0.02 * step).astype(jnp.bfloat16), m, v)  7.71 us

profile of v2, /device:TPU:2, one launch (start us, length us, event | category | flops | bytes accessed | tf_op | source)
XLA Modules:
  0.0 214.7 jit_solution(551037370174304292)
XLA Ops:
  0.6 206.3 %step.1 = (bf16[2,64,2048]{2,1,0:T(8,128)(2,1)}, bf16[2,64,2048]{2,1,0:T(8,128)(2,1)}, bf16[2,256,512]{2,1,0:T(8,128)(2,1)}) custom-call(bf16[2048,512]{1,0:T(8,128)(2,1)} %bitcast.2, bf16[2048,512]{1,0:T(8,128)(2,1)} %bitcast.3, bf16[2,64,2048]{2,1,0:T(8,128)(2,1)} %refs_2_.1, bf16[2,64,2048]{2,1,0:T(8,128)(2,1)} %refs_3_.1, bf16[2,256,512]{2,1,0:T(8,128)(2,1)} %refs_4_.1), custom_call_target="tpu_custom_call" | custom-call | tf_op jit(solution)/shard_map/step/pallas_call | solution.py:754
  206.9 0.0 copy-start
  206.9 0.0 copy-start.1
  206.9 0.0 copy-start.2
  206.9 0.0 copy-start.3
  206.9 5.9 %fusion.2 = (bf16[2,64,2048]{2,1,0:T(8,128)(2,1)}, f32[2,64,2048]{2,1,0:T(8,128)}, f32[2,64,2048]{2,1,0:T(8,128)}, bf16[2,64,2048]{2,1,0:T(8,128)(2,1)}, f32[2,64,2048]{2,1,0:T(8,128)}, /*index=5*/f32[2,64,2048]{2,1,0:T(8,128)}) fusion(bf16[2,64,2048]{2,1,0:T(8,128)(2,1)} %refs_2_.1, bf16[2,64,2048]{2,1,0:T(8,128)(2,1)} %get-tuple-element.12, ...), kind=kLoop, calls=%fused_computation.14 | loop fusion | flops 8388608 | bytes 11534336 | tf_op jit(solution)/shard_map/convert_element_type | solution.py:21
  212.8 0.0 copy-done
  212.8 0.0 copy-done.1
  212.8 0.0 copy-done.2
  212.9 0.0 copy-done.3
  212.9 1.8 fusion.10
Async XLA Ops:
  206.9 5.9 %copy-start = (bf16[2,256,512]{2,1,0:T(8,128)(2,1)S(1)}, bf16[2,256,512]{2,1,0:T(8,128)(2,1)}, u32[]{:S(2)}) copy-start(bf16[2,256,512]{2,1,0:T(8,128)(2,1)} %refs_4_.1) | copy-start | bytes 1572868
  206.9 5.9 %copy-start.1 = (f32[2,256,512]{2,1,0:T(8,128)S(1)}, f32[2,256,512]{2,1,0:T(8,128)}, u32[]{:S(2)}) copy-start(f32[2,256,512]{2,1,0:T(8,128)} %param.21) | copy-start | bytes 3145732
  206.9 5.9 %copy-start.2 = (f32[2,256,512]{2,1,0:T(8,128)S(1)}, f32[2,256,512]{2,1,0:T(8,128)}, u32[]{:S(2)}) copy-start(f32[2,256,512]{2,1,0:T(8,128)} %param.18) | copy-start | bytes 3145732
  206.9 5.9 %copy-start.3 = (bf16[2,256,512]{2,1,0:T(8,128)(2,1)S(1)}, bf16[2,256,512]{2,1,0:T(8,128)(2,1)}, u32[]{:S(2)}) copy-start(bf16[2,256,512]{2,1,0:T(8,128)(2,1)} %get-tuple-element.14) | copy-start | bytes 1572868
